TPU v7x, 32 devices: a whole 2x2x4 slice. The times are simulated.
32 devices in a mesh: blk: 4 (over y, x), grp: 8 (over z, core).
Axes of the slice: x: 2, y: 2, z: 4, core: 2. Of those that a mesh axis runs over, the one named last changes fastest.
Arguments:
- points: float32 [3, 4096], P(None, ('blk', 'grp')), may hold values from 0 to 1
- labels: int32 [4096], P(('blk', 'grp')), may hold values 0 or 1
- shape_scale: float32 [4096], P(('blk', 'grp')), may hold values from 0.1 to 0.4
- krylov_basis: float32 [8, 32, 4096], P(None, None, ('blk', 'grp')), may hold values from -6 to 6
- sketch: float32 [1024, 4096], P(None, ('blk', 'grp')), may hold values from -0.09375 to 0.09375
- sketched_basis: float32 [8, 32, 1024], replicated, may hold values from -0.1875 to 0.1875
Outputs:
- next_vector: float32 [32, 4096], P(None, ('blk', 'grp'))
- coefficients: float32 [8, 32], replicated
- sketch_next: float32 [32, 1024], replicated
- norms: float32 [32], replicated
All inputs are finite; a program needn't handle non-finite values. No bound on the sum of `labels` on one device may be relied on, other than what follows from the above.
Results may differ from a plain program's by a relative error of at most 0.0003.
Values sent between devices are 32-bit elements; how exact they have to be, the bound alone decides.
A program may use at most 64 MiB of HBM per device.

v0:
```python
import math
import jax
import jax.numpy as jnp
from jax import lax
from jax.sharding import PartitionSpec as P

SYSTEMS = 32
KRYLOV = 8


def kernel_terms(target_points, target_labels, source_block):
    source_points = source_block[0:3]
    scales = source_block[3]
    weights_block = source_block[4:]
    delta_x = source_points[0][:, None] - target_points[0][None, :]
    delta_y = source_points[1][:, None] - target_points[1][None, :]
    delta_z = source_points[2][:, None] - target_points[2][None, :]
    radius_sq = delta_x * delta_x + delta_y * delta_y + delta_z * delta_z
    squared_scale = (scales * scales)[:, None]
    shifted = radius_sq + squared_scale
    inverse = lax.rsqrt(shifted)
    boundary = shifted * inverse
    interior = (3.0 * squared_scale + 2.0 * radius_sq) * inverse * inverse * inverse
    kernel = jnp.where(target_labels[None, :] == 1, interior, boundary)
    return jnp.dot(
        weights_block, kernel, precision=lax.Precision.HIGHEST, preferred_element_type=jnp.float32
    )


def block_size(length, wanted):
    return wanted if length % wanted == 0 else length


def accumulate(running, target_points, target_labels, source_block):
    target_count = target_points.shape[1]
    source_count = source_block.shape[1]
    tblock = block_size(target_count, 2048)
    sblock = block_size(source_count, 2048)
    system_rows = running.shape[0]

    def over_targets(target_index, current):

        def over_sources(source_index, partial_value):
            portion = lax.dynamic_slice_in_dim(source_block, source_index * sblock, sblock, 1)
            return partial_value + kernel_terms(target_points, target_labels, portion)

        partial_value = lax.fori_loop(
            0, source_count // sblock, over_sources, jnp.zeros((system_rows, tblock), jnp.float32)
        )
        return current + partial_value

    return lax.fori_loop(0, target_count // tblock, over_targets, running)


def shards(points, labels, shape_scale, krylov_basis, sketch, sketched_basis):
    own_count = points.shape[1]
    everything = lax.axis_size("blk") * lax.axis_size("grp") * own_count
    sources = jnp.concatenate([points, shape_scale[None, :], krylov_basis[KRYLOV - 1]], axis=0)
    empty = jnp.zeros((SYSTEMS, own_count), jnp.float32)
    summed = accumulate(
        empty, points, labels, lax.all_gather(sources, ("blk", "grp"), axis=1, tiled=True)
    )
    image = summed / math.sqrt(everything)
    local_sketch = lax.dot_general(
        image,
        sketch,
        (((1,), (1,)), ((), ())),
        precision=lax.Precision.HIGHEST,
        preferred_element_type=jnp.float32,
    )
    sketched = lax.psum(local_sketch, ("blk", "grp"))
    coefficients = jnp.einsum(
        "jrk,rk->jr", sketched_basis, sketched, precision=lax.Precision.HIGHEST
    )
    remainder = sketched - jnp.einsum(
        "jr,jrk->rk", coefficients, sketched_basis, precision=lax.Precision.HIGHEST
    )
    norms = jnp.sqrt(jnp.mean(remainder * remainder, axis=1) + 1e-06)
    sketch_next = remainder / norms[:, None]
    reduced = image - jnp.einsum(
        "jr,jrn->rn", coefficients, krylov_basis, precision=lax.Precision.HIGHEST
    )
    next_vector = reduced / norms[:, None]
    return (next_vector, coefficients, sketch_next, norms)


def solution(mesh):
    placed = (
        P(None, ("blk", "grp")),
        P(("blk", "grp")),
        P(("blk", "grp")),
        P(None, None, ("blk", "grp")),
        P(None, ("blk", "grp")),
        P(),
    )
    return jax.shard_map(
        shards,
        mesh=mesh,
        in_specs=placed,
        out_specs=(P(None, ("blk", "grp")), P(), P(), P()),
        check_vma=False,
    )
```

profile of v0, /device:TPU:0, one launch (start us, length us, event | category | flops | bytes accessed | tf_op | source)
XLA Modules:
  0.0 195.9 jit_solution(17373773227067051160)
XLA Ops:
  7.2 0.0 copy-start
  7.2 0.0 all-reduce.2.cloned.1.call-start
  7.2 0.0 copy-start.4
  7.2 0.8 slice_bitcast_fusion.3
  8.0 0.0 copy-start.7
  8.1 0.0 copy-done.4
  8.1 0.7 copy-done.7
  8.7 45.9 %all_gather.3 = f32[36,4096]{1,0:T(8,128)S(1)} all-gather(f32[36,128]{1,0:T(8,128)S(1)} %pad_maximum_fusion), channel_id=1, replica_groups=mesh['blk'=4,'grp'=8] {'blk','grp'}, dimensions={1}, use_global_device_ids=true | all-gather | bytes 608256 | tf_op jit(solution)/shard_map/all_gather | solution.py:61
  54.7 0.0 copy-done.8
  54.7 4.4 %while.21 = (s32[]{:T(128)}, f32[32,128]{1,0:T(8,128)S(1)}, f32[36,4096]{1,0:T(8,128)S(1)}, s32[128]{0:T(128)S(1)}, f32[3,128]{1,0:T(4,128)S(1)}, /*index=5*/s32...) while((s32[]{:T(128)}, f32[32,128]{1,0:T(8,128)S(1)}, ...), condition=%wide.region_1.0_spmd.clone, body=%wide.region_0.1_spmd.clone.sunk | while | flops 104870024 | bytes 423813 | solution.py:47
  54.7 0.1 constant_dynamic-slice_fusion.2
  54.8 2.0 %convolution_add_fusion.2 = f32[32,128]{1,0:T(8,128)S(1)} fusion(f32[2048]{0:T(1024)S(1)} %bitcast.42, f32[128]{0:T(128)S(1)} %get-tuple-element.195, f32[2048]{0:T(1024)S(1)} %bitcast.45, f32[128]{0:T(128)S(1)} %get-tuple-element.197, f32[2048]{0:T(1024)S(1)} %bitcast.44, f32[128]{0:T(128)S(1)} %get-tuple-element.199, f32[2048]{0:T(1024)S(1)} %bitcast.43, ...), kind=kOutput, calls=%fused_computation.2.clone.1 | convolution fusion | flops 104865792 | bytes 337929 | tf_op jit(solution)/shard_map/while/body/eval_jaxpr/while/body/eval_jaxpr/dot_general | solution.py:25
  56.9 0.1 constant_dynamic-slice_fusion.2
  57.0 2.0 %convolution_add_fusion.2 = f32[32,128]{1,0:T(8,128)S(1)} fusion(f32[2048]{0:T(1024)S(1)} %bitcast.42, f32[128]{0:T(128)S(1)} %get-tuple-element.195, f32[2048]{0:T(1024)S(1)} %bitcast.45, f32[128]{0:T(128)S(1)} %get-tuple-element.197, f32[2048]{0:T(1024)S(1)} %bitcast.44, f32[128]{0:T(128)S(1)} %get-tuple-element.199, f32[2048]{0:T(1024)S(1)} %bitcast.43, ...), kind=kOutput, calls=%fused_computation.2.clone.1 | convolution fusion | flops 104865792 | bytes 337929 | tf_op jit(solution)/shard_map/while/body/eval_jaxpr/while/body/eval_jaxpr/dot_general | solution.py:25
  59.1 0.0 copy-done.2
  59.1 1.3 fusion.32
  60.3 0.0 all-reduce.2.cloned.1.call-update
  60.4 120.9 %all-reduce.2.cloned.1.call-done = f32[32,1024]{1,0:T(8,128)} async-done(((f32[32,1024]{1,0:T(8,128)}), f32[32,1024]{1,0:T(8,128)}) %all-reduce.2.cloned.1.call-update) | async-done | bytes 131088 | tf_op jit(solution)/shard_map/psum | solution.py:71
  181.2 0.0 copy-done
  181.3 3.6 %fusion.27 = f32[32,1,8]{2,1,0:T(1,128)S(1)} fusion(f32[8,32,1024]{2,1,0:T(8,128)S(1)} %copy-done, f32[32,1024,1]{1,0,2:T(8,128)} %bitcast.40), kind=kOutput, calls=%fused_computation.36 | convolution fusion | flops 3145728 | bytes 1180672 | tf_op jit(solution)/shard_map/jrk,rk->jr/dot_general | solution.py:72
  184.8 0.1 copy.12
  184.9 0.1 copy.13
  185.0 0.5 copy-done.5
  185.5 0.0 copy-done.3
  185.5 0.4 fusion.29
  185.9 0.0 copy-start.1
  185.9 1.5 fusion.25
  187.4 0.0 copy-done.1
  187.4 0.1 multiply_reduce_fusion
  187.6 0.7 subtract_divide_fusion
  188.3 0.0 copy-done.6
  188.3 0.7 broadcast_divide_fusion
  (14 shorter events, 0.1 us)
Async XLA Ops:
  7.2 174.1 %copy-start = (f32[8,32,1024]{2,1,0:T(8,128)S(1)}, f32[8,32,1024]{2,1,0:T(8,128)}, u32[]{:S(2)}) copy-start(f32[8,32,1024]{2,1,0:T(8,128)} %param.13) | copy-start | bytes 3145732
  7.2 174.1 %all-reduce.2.cloned.1.call-start = ((), (), s32[]{:S(2)}) async-start(), calls=%async_computation | async-start | bytes 262144 | tf_op jit(solution)/shard_map/psum | solution.py:71
  7.2 0.8 copy-start.4
  8.0 0.7 copy-start.7
  8.7 46.0 %copy-start.8 = (s32[128]{0:T(128)S(1)}, s32[128]{0:T(128)}, u32[]{:S(2)}) copy-start(s32[128]{0:T(128)} %param.9) | copy-start | bytes 1540
  54.7 4.4 %copy-start.2 = (f32[1024,128]{1,0:T(8,128)S(1)}, f32[1024,128]{1,0:T(8,128)}, u32[]{:S(2)}) copy-start(f32[1024,128]{1,0:T(8,128)} %param.12) | copy-start | bytes 1572868
  181.2 4.3 %copy-start.3 = (f32[8,32,128]{2,1,0:T(8,128)S(1)}, f32[8,32,128]{2,1,0:T(8,128)}, u32[]{:S(2)}) copy-start(f32[8,32,128]{2,1,0:T(8,128)} %param.11) | copy-start | bytes 393220
  184.9 0.6 copy-start.5
  185.9 1.5 copy-start.1
  187.6 0.7 copy-start.6
Sparse Core Ops, SparseCore 0:
  60.5 120.7 all-reduce.1
where the time goes:
time: 196 us
  waiting for transfers between devices  121 us (62%)
  blocking collectives  45.9 us (23%)
  between operations  14.1 us (7%)
  matrix products  10.7 us (5%)
  local copies, waits for them, and re-layouts  2.17 us (1%)
    psum x1, waiting for transfers between devices, shards(): sketched = lax.psum(local_sketch, ('blk', 'grp'))  121 us
    all_gather x1, blocking collectives, shards(): lax.all_gather(sources, ('blk', 'grp'), axis=1, tiled=True)  45.9 us
    dot_general x2, matrix products, kernel_terms(): jnp.dot(weights_block, kernel, precision=lax.Precision.HIGHEST, preferred...  4 us
  transfers between devices with their start and end apart: 1, of which 1 were waited for; matrix products, arithmetic and copies ran while one was open for 0% of the time, Pallas kernels for 0%

commit v1 on v0

--- a/solution.py
+++ b/solution.py
@@ -3,6 +3,7 @@
 import jax.numpy as jnp
 from jax import lax
 from jax.sharding import PartitionSpec as P
+from jax.lax import psum
 
 SYSTEMS = 32
 KRYLOV = 8
@@ -68,7 +69,13 @@
         precision=lax.Precision.HIGHEST,
         preferred_element_type=jnp.float32,
     )
-    sketched = lax.psum(local_sketch, ("blk", "grp"))
+
+    def racks_track(w_in):
+        for ii in ("grp", "blk"):
+            w_in = psum(w_in, axis_name=ii)
+        return w_in
+
+    sketched = racks_track(local_sketch)
     coefficients = jnp.einsum(
         "jrk,rk->jr", sketched_basis, sketched, precision=lax.Precision.HIGHEST
     )

time: 196 us -> 171 us (0.87)
  waiting for transfers between devices: 121 us -> 95.5 us
    psum x1 -> x2, waiting for transfers between devices: 121 us -> 95.5 us  [racks_track(): w_in = psum(w_in, axis_name=ii)]
  transfers between devices with their start and end apart: 1 -> 2, of which waited for: 1 -> 2; matrix products, arithmetic and copies ran while one was open for 0% -> 0% of each run, Pallas kernels for 0% -> 0%
where the time goes in v1:
time: 171 us
  waiting for transfers between devices  95.5 us (56%)
  blocking collectives  45.9 us (27%)
  between operations  14.1 us (8%)
  matrix products  10.7 us (6%)
  local copies, waits for them, and re-layouts  2.17 us (1%)
  other arithmetic  1.87 us (1%)
    psum x2, waiting for transfers between devices, racks_track(): w_in = psum(w_in, axis_name=ii)  95.5 us
    all_gather x1, blocking collectives, shards(): lax.all_gather(sources, ('blk', 'grp'), axis=1, tiled=True)  45.9 us
    dot_general x2, matrix products, kernel_terms(): jnp.dot(weights_block, kernel, precision=lax.Precision.HIGHEST, preferred...  4 us
    dot_general x1, matrix products, shards(): jnp.einsum('jrk,rk->jr', sketched_basis, sketched, precision=lax.Precisio...  3.57 us
  transfers between devices with their start and end apart: 2, of which 2 were waited for; matrix products, arithmetic and copies ran while one was open for 0% of the time, Pallas kernels for 0%

profile of v1, /device:TPU:0, one launch (start us, length us, event | category | flops | bytes accessed | tf_op | source)
XLA Modules:
  0.0 170.5 jit_solution(13232438662401297790)
XLA Ops:
  7.2 0.0 copy-start
  7.2 0.0 all-reduce.3.cloned.1.call-start
  7.2 0.0 copy-start.4
  7.2 0.8 slice_bitcast_fusion.3
  8.1 0.0 copy-done.4
  8.1 0.7 copy-done.7
  8.7 45.9 %all_gather.3 = f32[36,4096]{1,0:T(8,128)S(1)} all-gather(f32[36,128]{1,0:T(8,128)S(1)} %pad_maximum_fusion), channel_id=1, replica_groups=mesh['blk'=4,'grp'=8] {'blk','grp'}, dimensions={1}, use_global_device_ids=true | all-gather | bytes 608256 | tf_op jit(solution)/shard_map/all_gather | solution.py:62
  54.7 0.0 copy-done.8
  54.7 4.4 %while.21 = (s32[]{:T(128)}, f32[32,128]{1,0:T(8,128)S(1)}, f32[36,4096]{1,0:T(8,128)S(1)}, s32[128]{0:T(128)S(1)}, f32[3,128]{1,0:T(4,128)S(1)}, /*index=5*/s32...) while((s32[]{:T(128)}, f32[32,128]{1,0:T(8,128)S(1)}, ...), condition=%wide.region_1.0_spmd.clone, body=%wide.region_0.1_spmd.clone.sunk | while | flops 104870024 | bytes 423813 | solution.py:48
  54.7 0.1 constant_dynamic-slice_fusion.2
  54.8 2.0 %convolution_add_fusion.2 = f32[32,128]{1,0:T(8,128)S(1)} fusion(f32[2048]{0:T(1024)S(1)} %bitcast.42, f32[128]{0:T(128)S(1)} %get-tuple-element.195, f32[2048]{0:T(1024)S(1)} %bitcast.45, f32[128]{0:T(128)S(1)} %get-tuple-element.197, f32[2048]{0:T(1024)S(1)} %bitcast.44, f32[128]{0:T(128)S(1)} %get-tuple-element.199, f32[2048]{0:T(1024)S(1)} %bitcast.43, ...), kind=kOutput, calls=%fused_computation.2.clone.1 | convolution fusion | flops 104865792 | bytes 337929 | tf_op jit(solution)/shard_map/while/body/eval_jaxpr/while/body/eval_jaxpr/dot_general | solution.py:26
  56.9 0.1 constant_dynamic-slice_fusion.2
  57.0 2.0 %convolution_add_fusion.2 = f32[32,128]{1,0:T(8,128)S(1)} fusion(f32[2048]{0:T(1024)S(1)} %bitcast.42, f32[128]{0:T(128)S(1)} %get-tuple-element.195, f32[2048]{0:T(1024)S(1)} %bitcast.45, f32[128]{0:T(128)S(1)} %get-tuple-element.197, f32[2048]{0:T(1024)S(1)} %bitcast.44, f32[128]{0:T(128)S(1)} %get-tuple-element.199, f32[2048]{0:T(1024)S(1)} %bitcast.43, ...), kind=kOutput, calls=%fused_computation.2.clone.1 | convolution fusion | flops 104865792 | bytes 337929 | tf_op jit(solution)/shard_map/while/body/eval_jaxpr/while/body/eval_jaxpr/dot_general | solution.py:26
  59.1 0.0 copy-done.2
  59.1 1.3 fusion.32
  60.3 0.0 all-reduce.3.cloned.1.call-update
  60.4 0.0 all-reduce.5.cloned.1.call-start
  60.4 51.3 %all-reduce.3.cloned.1.call-done = f32[32,1024]{1,0:T(8,128)} async-done(((f32[32,1024]{1,0:T(8,128)}), f32[32,1024]{1,0:T(8,128)}) %all-reduce.3.cloned.1.call-update) | async-done | bytes 131088 | tf_op jit(solution)/shard_map/psum | solution.py:75
  111.7 0.0 all-reduce.5.cloned.1.call-update
  111.7 44.2 %all-reduce.5.cloned.1.call-done = f32[32,1024]{1,0:T(8,128)} async-done(((f32[32,1024]{1,0:T(8,128)}), f32[32,1024]{1,0:T(8,128)}) %all-reduce.5.cloned.1.call-update) | async-done | bytes 131088 | tf_op jit(solution)/shard_map/psum | solution.py:75
  155.9 0.0 copy-done
  155.9 3.6 %fusion.27 = f32[32,1,8]{2,1,0:T(1,128)S(1)} fusion(f32[8,32,1024]{2,1,0:T(8,128)S(1)} %copy-done, f32[32,1024,1]{1,0,2:T(8,128)} %bitcast.40), kind=kOutput, calls=%fused_computation.36 | convolution fusion | flops 3145728 | bytes 1180672 | tf_op jit(solution)/shard_map/jrk,rk->jr/dot_general | solution.py:79
  159.5 0.1 copy.12
  159.5 0.1 copy.13
  159.6 0.5 copy-done.5
  160.1 0.0 copy-done.3
  160.1 0.4 fusion.29
  160.6 1.5 fusion.25
  162.1 0.1 multiply_reduce_fusion
  162.2 0.7 subtract_divide_fusion
  162.9 0.0 copy-done.6
  162.9 0.7 broadcast_divide_fusion
  (17 shorter events, 0.1 us)
Async XLA Ops:
  7.2 148.7 %copy-start = (f32[8,32,1024]{2,1,0:T(8,128)S(1)}, f32[8,32,1024]{2,1,0:T(8,128)}, u32[]{:S(2)}) copy-start(f32[8,32,1024]{2,1,0:T(8,128)} %param.13) | copy-start | bytes 3145732
  7.2 104.5 %all-reduce.3.cloned.1.call-start = ((), (), s32[]{:S(2)}) async-start(), calls=%async_computation | async-start | bytes 262144 | tf_op jit(solution)/shard_map/psum | solution.py:75
  7.2 0.8 copy-start.4
  8.0 0.7 copy-start.7
  8.7 46.0 %copy-start.8 = (s32[128]{0:T(128)S(1)}, s32[128]{0:T(128)}, u32[]{:S(2)}) copy-start(s32[128]{0:T(128)} %param.9) | copy-start | bytes 1540
  54.7 4.4 %copy-start.2 = (f32[1024,128]{1,0:T(8,128)S(1)}, f32[1024,128]{1,0:T(8,128)}, u32[]{:S(2)}) copy-start(f32[1024,128]{1,0:T(8,128)} %param.12) | copy-start | bytes 1572868
  60.4 95.5 %all-reduce.5.cloned.1.call-start = ((), (), s32[]{:S(2)}) async-start(), calls=%async_computation.1 | async-start | bytes 262144 | tf_op jit(solution)/shard_map/psum | solution.py:75
  155.9 4.3 %copy-start.3 = (f32[8,32,128]{2,1,0:T(8,128)S(1)}, f32[8,32,128]{2,1,0:T(8,128)}, u32[]{:S(2)}) copy-start(f32[8,32,128]{2,1,0:T(8,128)} %param.11) | copy-start | bytes 393220
  159.5 0.6 copy-start.5
  160.6 1.5 copy-start.1
  162.2 0.7 copy-start.6
Sparse Core Ops, SparseCore 0:
  60.5 51.1 all-reduce.2
  114.6 41.2 all-reduce.4
